TPU v7x, 128 devices: a whole 4x4x4 slice. The times are simulated.
128 devices in a mesh: dp: 8 (over x, core), expert: 16 (over y, z).
Axes of the slice: x: 4, y: 4, z: 4, core: 2. Of those that a mesh axis runs over, the one named last changes fastest.
Arguments:
- grads: bfloat16 [131072, 4096], P(('dp', 'expert')), may hold values from -6 to 6
- block_expert: int32 [1024, 1], P(('dp', 'expert')), may hold values from 0 to 15; in each aligned block of 8 rows (0 to 7, 8 to 15, ...) at most 2 rows name the same one
- sketch: bfloat16 [16, 256, 4096], P('expert', None, 'dp'), may hold values from -0.09375 to 0.09375
Outputs:
- factor: bfloat16 [16, 256, 4096], P('expert')
Inputs may be any that keep to these rules, and one draw needn't show every extreme that they name: `block_expert`: among the 8 blocks of one device, at most 2 belong to one expert, and every expert has some block.
All inputs are finite; a program needn't handle non-finite values.
Results may differ from a plain program's by a relative error of at most 0.0031.
Values may be sent and summed in bfloat16 or wider, within the bound.
A program may use at most 256 MiB of HBM per device.

v0:
```python
import jax
import jax.numpy as jnp
from jax import lax
from jax.sharding import PartitionSpec as P

D = 4096
BLOCK = 128
CAP = 2
ITERS = 5
EPSILON = 1e-06


def in_blocks(x, dim, length):
    lengths = x.shape
    parts = x.reshape(*lengths[:dim], length, lengths[dim] // length, *lengths[dim + 1 :])
    return jnp.moveaxis(parts, dim, 0)


def cut_rows(length, count):
    turn = length // count
    if turn >= 8:
        turn -= turn % 8
    return [turn * k for k in range(1, count)]


def laid_out(parts, dim):
    parts = jnp.moveaxis(parts, 0, dim)
    lengths = parts.shape
    return parts.reshape(*lengths[:dim], lengths[dim] * lengths[dim + 1], *lengths[dim + 2 :])


def cut_exchange(x, axis, pieces, split_dim, concat_dim):
    parts = in_blocks(x, split_dim, lax.axis_size(axis))
    split_at = max(range(1, max(2, parts.ndim - 1)), key=lambda d: parts.shape[d])
    gathered = []
    for piece in jnp.split(parts, cut_rows(parts.shape[split_at], pieces), axis=split_at):
        if piece.size:
            gathered.append(lax.all_to_all(piece, axis, split_axis=0, concat_axis=0, tiled=True))
    return laid_out(jnp.concatenate(gathered, axis=split_at), concat_dim)


def newton_step(iterate, inner):
    return 1.5 * iterate - 0.5 * jnp.dot(inner, iterate, precision=lax.Precision.HIGHEST)


def shards(grads, block_expert, sketch):
    count_blocks = block_expert.shape[0]
    columns = grads.shape[1]
    experts = lax.axis_size("expert")
    replicas = lax.axis_size("dp")
    blocks = grads.reshape(count_blocks, BLOCK, columns)
    owners = block_expert[:, 0]
    same_owner = owners[None, :] == owners[:, None]
    earlier = lax.broadcasted_iota(
        jnp.int32, (count_blocks, count_blocks), 1
    ) < lax.broadcasted_iota(jnp.int32, (count_blocks, count_blocks), 0)
    places = jnp.sum((same_owner & earlier).astype(jnp.int32), axis=1)
    targets = owners * CAP + places
    outgoing = jnp.zeros((experts * CAP, BLOCK, columns), jnp.bfloat16).at[targets].set(blocks)
    outgoing = outgoing.reshape(experts, CAP * BLOCK, columns)
    incoming = cut_exchange(outgoing, "expert", 2, 0, 0)
    arrived = incoming.reshape(experts * CAP * BLOCK, columns)
    basis_full = lax.all_gather(sketch, "dp", axis=2, tiled=True)[0]
    projected = lax.dot_general(
        basis_full, arrived, (((1,), (1,)), ((), ())), preferred_element_type=jnp.float32
    ).astype(jnp.bfloat16)
    partial_term = jnp.dot(projected, arrived, preferred_element_type=jnp.float32)
    basis_gram = lax.dot_general(
        basis_full, basis_full, (((1,), (1,)), ((), ())), preferred_element_type=jnp.float32
    )
    average = float(BLOCK * count_blocks * replicas)
    gradient_term = lax.psum(partial_term, "dp")
    unscaled = (
        jnp.dot(basis_gram, basis_full.astype(jnp.float32), precision=lax.Precision.HIGHEST)
        + gradient_term / average
    )
    iterate = unscaled / jnp.sqrt(jnp.sum(unscaled * unscaled) + EPSILON)
    for step in range(ITERS):
        inner = lax.dot_general(
            iterate, iterate, (((1,), (1,)), ((), ())), precision=lax.Precision.HIGHEST
        )
        iterate = newton_step(iterate, inner)
    return (iterate * D**0.5).astype(jnp.bfloat16)[None]


def solution(mesh):
    in_specs = (P(("dp", "expert"), None), P(("dp", "expert"), None), P("expert", None, "dp"))
    out_specs = P("expert", None, None)
    return jax.shard_map(shards, mesh=mesh, in_specs=in_specs, out_specs=out_specs, check_vma=False)
```

profile of v0, /device:TPU:0, one launch (start us, length us, event | category | flops | bytes accessed | tf_op | source)
XLA Modules:
  0.0 766.7 jit_solution(16272449002042471784)
XLA Ops:
  6.5 0.9 convert_reduce_fusion
  7.4 0.7 fusion.16
  8.1 11.0 %broadcast_in_dim.7 = bf16[32,128,4096]{2,1,0:T(8,128)(2,1)} broadcast(bf16[]{:T(256)} %constant.10.clone.1), dimensions={} | broadcast | bytes 33554432 | tf_op jit(solution)/shard_map/broadcast_in_dim | solution.py:59
  19.1 21.4 %scatter_fusion = bf16[32,128,4096]{2,1,0:T(8,128)(2,1)} fusion(bf16[32,128,4096]{2,1,0:T(8,128)(2,1)} %broadcast_in_dim.7, s32[8]{0:T(128)S(1)} %fusion.16, bf16[8,128,4096]{2,1,0:T(8,128)(2,1)} %bitcast.44), kind=kCustom, calls=%fused_computation | custom fusion | bytes 25165856 | tf_op jit(solution)/shard_map/scatter | solution.py:59
  40.5 18.2 %fusion.17 = (bf16[16,1,128,4096]{3,2,1,0:T(8,128)(2,1)S(1)}, bf16[16,1,128,4096]{3,2,1,0:T(8,128)(2,1)}) fusion(bf16[16,1,256,4096]{3,2,1,0:T(8,128)(2,1)} %bitcast.42), kind=kLoop, calls=%fused_computation.31 | loop fusion | bytes 67108864 | tf_op jit(solution)/shard_map/split | solution.py:36
  58.7 195.6 %all_to_all.10 = bf16[16,1,128,4096]{3,2,1,0:T(8,128)(2,1)} all-to-all(bf16[16,1,128,4096]{3,2,1,0:T(8,128)(2,1)S(1)} %get-tuple-element.5), channel_id=1, replica_groups=mesh['dp'=8,'expert'=16] {'expert'}, dimensions={0} | all-to-all | bytes 33554432 | tf_op jit(solution)/shard_map/all_to_all | solution.py:38
  254.3 5.1 all-to-all-start.1
  259.4 0.0 all-gather.2.cloned.1.call-start
  259.5 0.7 all-gather.2.cloned.1.call-update
  260.1 0.0 all-reduce.2.cloned.1.call-start
  260.2 296.6 %all-to-all-done.1 = bf16[16,1,128,4096]{3,2,1,0:T(8,128)(2,1)} async-done(((bf16[16,1,128,4096]{3,2,1,0:T(8,128)(2,1)}), bf16[16,1,128,4096]{3,2,1,0:T(8,128)(2,1)}, u32[]{:S(2)}, u32[]{:S(2)}) %all-to-all-start.1) | async-done | bytes 16777248 | tf_op jit(solution)/shard_map/all_to_all | solution.py:38
  556.8 22.8 %pad_maximum_fusion = bf16[16,1,256,4096]{3,2,1,0:T(8,128)(2,1)} fusion(bf16[16,1,128,4096]{3,2,1,0:T(8,128)(2,1)} %all-to-all-done.1, bf16[16,1,128,4096]{3,2,1,0:T(8,128)(2,1)} %all_to_all.10), kind=kLoop, calls=%fused_computation.1 | loop fusion | flops 67108864 | bytes 67108864 | tf_op jit(solution)/shard_map/concatenate | solution.py:39
  579.6 0.0 all-gather.2.cloned.1.call-done
  579.6 47.4 %fusion.8 = f32[256,4096]{1,0:T(8,128)} fusion(bf16[4096,4096]{1,0:T(8,128)(2,1)} %bitcast.43, bf16[1,256,4096]{2,1,0:T(8,128)(2,1)} %all-gather.2.cloned.1.call-done), kind=kOutput, calls=%fused_computation.18 | convolution fusion | flops 17180917760 | bytes 39845888 | tf_op jit(solution)/shard_map/dot_general | solution.py:67
  627.0 0.0 copy-start.1
  627.0 0.0 all-reduce.2.cloned.1.call-update
  627.0 1.6 copy-done.1
  628.6 0.7 fusion.12
  629.3 73.8 %all-reduce.2.cloned.1.call-done = f32[256,4096]{1,0:T(8,128)} async-done(((f32[256,4096]{1,0:T(8,128)}), f32[256,4096]{1,0:T(8,128)}) %all-reduce.2.cloned.1.call-update) | async-done | bytes 4194320 | tf_op jit(solution)/shard_map/psum | solution.py:72
  703.1 7.3 multiply_reduce_fusion
  711.1 0.0 copy-start
  711.1 12.2 %fusion.14 = f32[256,256]{1,0:T(8,128)S(1)} fusion(f32[256,4096]{1,0:T(8,128)} %get-tuple-element.8, f32[]{:T(128)S(6)} %sqrt.3), kind=kOutput, calls=%fused_computation.24 | convolution fusion | flops 3222274048 | bytes 4456452 | tf_op jit(solution)/shard_map/dot_general | solution.py:79
  723.3 0.0 copy-done
  723.3 4.1 fusion.4
  727.5 3.5 fusion.18
  731.0 4.1 fusion.3
  735.1 3.9 fusion.19
  739.1 4.1 fusion.2
  743.2 3.5 fusion.20
  746.7 4.3 fusion.1
  751.0 3.5 fusion.21
  754.6 5.1 fusion.7
Async XLA Ops:
  254.3 302.5 %all-to-all-start.1 = ((bf16[16,1,128,4096]{3,2,1,0:T(8,128)(2,1)}), bf16[16,1,128,4096]{3,2,1,0:T(8,128)(2,1)}, u32[]{:S(2)}, u32[]{:S(2)}) async-start(bf16[16,1,128,4096]{3,2,1,0:T(8,128)(2,1)} %get-tuple-element.6), calls=%async_computation.1 | async-start | bytes 33554432 | tf_op jit(solution)/shard_map/all_to_all | solution.py:38
  259.4 320.2 %all-gather.2.cloned.1.call-start = ((), (), s32[]{:S(2)}) async-start(), calls=%async_computation.2 | async-start | bytes 2359296 | tf_op jit(solution)/shard_map/all_gather | solution.py:63
  260.1 443.0 %all-reduce.2.cloned.1.call-start = ((), (), s32[]{:S(2)}) async-start(), calls=%async_computation.3 | async-start | bytes 8388608 | tf_op jit(solution)/shard_map/psum | solution.py:72
  627.0 1.6 copy-start.1
  711.1 12.2 %copy-start = (f32[256,4096]{1,0:T(8,128)S(1)}, f32[256,4096]{1,0:T(8,128)}, u32[]{:S(2)}) copy-start(f32[256,4096]{1,0:T(8,128)} %get-tuple-element.8) | copy-start | bytes 12582916
Sparse Core Ops, SparseCore 0:
  261.9 26.6 all-gather.1
  627.2 75.9 all-reduce.1
where the time goes:
time: 775 us; the launch traced here: 767 us
  waiting for transfers between devices  371 us (48%)
  blocking collectives  196 us (25%)
  matrix products  104 us (13%)
  local copies, waits for them, and re-layouts  52.2 us (7%)
  other arithmetic  24.4 us (3%)
  between operations  14.4 us (2%)
    all_to_all x1, waiting for transfers between devices, cut_exchange(): lax.all_to_all(piece, axis, split_axis=0, concat_axis=0, tiled=True)  297 us
    all_to_all x1, blocking collectives, cut_exchange(): lax.all_to_all(piece, axis, split_axis=0, concat_axis=0, tiled=True)  196 us
    psum x1, waiting for transfers between devices, shards(): gradient_term = lax.psum(partial_term, 'dp')  73.8 us
    dot_general x1, matrix products, shards(): jnp.dot(projected, arrived, preferred_element_type=jnp.float32)  47.4 us
    dot_general x5, matrix products, shards(): lax.dot_general(iterate, iterate, (((1,), (1,)), ((), ())), precision=lax...  26.8 us
    concatenate x1, other arithmetic, cut_exchange(): return laid_out(jnp.concatenate(gathered, axis=split_at), concat_dim)  22.8 us
    dot_general x5, matrix products, newton_step(): jnp.dot(inner, iterate, precision=lax.Precision.HIGHEST)  21.7 us
    scatter x1, local copies, waits for them, and re-layouts, shards(): jnp.zeros((experts * CAP, BLOCK, columns), jnp.bfloat16).at[targets]  21.4 us
  transfers between devices with their start and end apart: 3, of which 2 were waited for; matrix products, arithmetic and copies ran while one was open for 3% of the time, Pallas kernels for 0%

commit v1 on v0

--- a/solution.py
+++ b/solution.py
@@ -69,7 +69,14 @@
         basis_full, basis_full, (((1,), (1,)), ((), ())), preferred_element_type=jnp.float32
     )
     average = float(BLOCK * count_blocks * replicas)
-    gradient_term = lax.psum(partial_term, "dp")
+    axis_n = jax.lax.axis_size("dp")
+    gradient_term, far_arr = (partial_term, 0)
+    while 1 << far_arr < axis_n:
+        row_out = jax.lax.ppermute(
+            gradient_term, "dp", perm=[(dev_i, dev_i ^ 1 << far_arr) for dev_i in range(axis_n)]
+        )
+        gradient_term = gradient_term + row_out
+        far_arr = far_arr + 1
     unscaled = (
         jnp.dot(basis_gram, basis_full.astype(jnp.float32), precision=lax.Precision.HIGHEST)
         + gradient_term / average

time: 775 us -> 895 us (1.15)
  waiting for transfers between devices: 371 us -> 484 us
    ppermute x0 -> x3, waiting for transfers between devices: none -> 186 us  [shards(): jax.lax.ppermute(gradient_term, 'dp', perm=[(dev_i, dev_i ^ 1 << far_arr)...]
    psum x1 -> x0, waiting for transfers between devices: 73.8 us -> none  [shards(): gradient_term = lax.psum(partial_term, 'dp')]
  transfers between devices with their start and end apart: 3 -> 5, of which waited for: 2 -> 4; matrix products, arithmetic and copies ran while one was open for 3% -> 3% of each run, Pallas kernels for 0% -> 0%
where the time goes in v1:
time: 895 us; the launch traced here: 885 us
  waiting for transfers between devices  484 us (54%)
  blocking collectives  196 us (22%)
  matrix products  98.6 us (11%)
  local copies, waits for them, and re-layouts  50.6 us (6%)
  other arithmetic  31.9 us (4%)
  between operations  14.4 us (2%)
  starting transfers between devices  10.1 us (1%)
    all_to_all x1, waiting for transfers between devices, cut_exchange(): lax.all_to_all(piece, axis, split_axis=0, concat_axis=0, tiled=True)  297 us
    all_to_all x1, blocking collectives, cut_exchange(): lax.all_to_all(piece, axis, split_axis=0, concat_axis=0, tiled=True)  196 us
    ppermute x3, waiting for transfers between devices, shards(): jax.lax.ppermute(gradient_term, 'dp', perm=[(dev_i, dev_i ^ 1 << far_arr)...  186 us
    dot_general x1, matrix products, shards(): jnp.dot(projected, arrived, preferred_element_type=jnp.float32)  47.5 us
    dot_general x5, matrix products, shards(): lax.dot_general(iterate, iterate, (((1,), (1,)), ((), ())), precision=lax...  26.7 us
    concatenate x1, other arithmetic, cut_exchange(): return laid_out(jnp.concatenate(gathered, axis=split_at), concat_dim)  22.8 us
    dot_general x5, matrix products, newton_step(): jnp.dot(inner, iterate, precision=lax.Precision.HIGHEST)  21.7 us
    scatter x1, local copies, waits for them, and re-layouts, shards(): jnp.zeros((experts * CAP, BLOCK, columns), jnp.bfloat16).at[targets]  21.4 us
  transfers between devices with their start and end apart: 5, of which 4 were waited for; matrix products, arithmetic and copies ran while one was open for 3% of the time, Pallas kernels for 0%

profile of v1, /device:TPU:0, one launch (start us, length us, event | category | flops | bytes accessed | tf_op | source)
XLA Modules:
  0.0 884.9 jit_solution(834052321272674755)
XLA Ops:
  6.5 0.9 convert_reduce_fusion
  7.4 0.7 fusion.16
  8.1 11.0 %broadcast_in_dim.7 = bf16[32,128,4096]{2,1,0:T(8,128)(2,1)} broadcast(bf16[]{:T(256)} %constant.10.clone.1), dimensions={} | broadcast | bytes 33554432 | tf_op jit(solution)/shard_map/broadcast_in_dim | solution.py:59
  19.1 21.4 %scatter_fusion = bf16[32,128,4096]{2,1,0:T(8,128)(2,1)} fusion(bf16[32,128,4096]{2,1,0:T(8,128)(2,1)} %broadcast_in_dim.7, s32[8]{0:T(128)S(1)} %fusion.16, bf16[8,128,4096]{2,1,0:T(8,128)(2,1)} %bitcast.42), kind=kCustom, calls=%fused_computation | custom fusion | bytes 25165856 | tf_op jit(solution)/shard_map/scatter | solution.py:59
  40.5 18.2 %fusion.17 = (bf16[16,1,128,4096]{3,2,1,0:T(8,128)(2,1)S(1)}, bf16[16,1,128,4096]{3,2,1,0:T(8,128)(2,1)}) fusion(bf16[16,1,256,4096]{3,2,1,0:T(8,128)(2,1)} %bitcast.40), kind=kLoop, calls=%fused_computation.32 | loop fusion | bytes 67108864 | tf_op jit(solution)/shard_map/split | solution.py:36
  58.7 195.6 %all_to_all.10 = bf16[16,1,128,4096]{3,2,1,0:T(8,128)(2,1)} all-to-all(bf16[16,1,128,4096]{3,2,1,0:T(8,128)(2,1)S(1)} %get-tuple-element.7), channel_id=1, replica_groups=mesh['dp'=8,'expert'=16] {'expert'}, dimensions={0} | all-to-all | bytes 33554432 | tf_op jit(solution)/shard_map/all_to_all | solution.py:38
  254.2 5.1 all-to-all-start.1
  259.4 0.0 all-gather.2.cloned.1.call-start
  259.4 0.7 all-gather.2.cloned.1.call-update
  260.1 296.9 %all-to-all-done.1 = bf16[16,1,128,4096]{3,2,1,0:T(8,128)(2,1)} async-done(((bf16[16,1,128,4096]{3,2,1,0:T(8,128)(2,1)}), bf16[16,1,128,4096]{3,2,1,0:T(8,128)(2,1)}, u32[]{:S(2)}, u32[]{:S(2)}) %all-to-all-start.1) | async-done | bytes 16777248 | tf_op jit(solution)/shard_map/all_to_all | solution.py:38
  557.1 22.8 %pad_maximum_fusion = bf16[16,1,256,4096]{3,2,1,0:T(8,128)(2,1)} fusion(bf16[16,1,128,4096]{3,2,1,0:T(8,128)(2,1)} %all-to-all-done.1, bf16[16,1,128,4096]{3,2,1,0:T(8,128)(2,1)} %all_to_all.10), kind=kLoop, calls=%fused_computation.1 | loop fusion | flops 67108864 | bytes 67108864 | tf_op jit(solution)/shard_map/concatenate | solution.py:39
  579.9 47.5 %fusion.7 = f32[256,4096]{1,0:T(8,128)} fusion(bf16[4096,4096]{1,0:T(8,128)(2,1)} %bitcast.41, bf16[1,256,4096]{2,1,0:T(8,128)(2,1)} %all-gather.2.cloned.1.call-done), kind=kOutput, calls=%fused_computation.18 | convolution fusion | flops 17180917760 | bytes 39845888 | tf_op jit(solution)/shard_map/dot_general | solution.py:67
  627.4 7.4 collective-permute-done
  634.8 2.8 add.25
  637.5 1.6 collective-permute-start.1
  639.1 91.1 %collective-permute-done.1 = f32[256,4096]{1,0:T(8,128)S(1)} collective-permute-done((f32[256,4096]{1,0:T(8,128)S(1)}, f32[256,4096]{1,0:T(8,128)S(1)}, u32[]{:S(2)}, u32[]{:S(2)}) %collective-permute-start.1) | collective-permute-done | bytes 4194336 | tf_op jit(solution)/shard_map/ppermute | solution.py:75
  730.2 0.5 add.26
  730.7 3.3 collective-permute-start.2
  734.1 0.7 fusion.12
  734.8 1.9 fusion.10
  736.7 87.7 %collective-permute-done.2 = f32[256,4096]{1,0:T(8,128)S(1)} collective-permute-done((f32[256,4096]{1,0:T(8,128)S(1)}, f32[256,4096]{1,0:T(8,128)S(1)}, u32[]{:S(2)}, u32[]{:S(2)}) %collective-permute-start.2) | collective-permute-done | bytes 4194336 | tf_op jit(solution)/shard_map/ppermute | solution.py:75
  824.4 4.3 multiply_reduce_fusion
  829.3 12.2 %fusion.14 = f32[256,256]{1,0:T(8,128)S(1)} fusion(f32[256,4096]{1,0:T(8,128)} %get-tuple-element.6, f32[]{:T(128)S(6)} %sqrt.3), kind=kOutput, calls=%fused_computation.25 | convolution fusion | flops 3222274048 | bytes 4456452 | tf_op jit(solution)/shard_map/dot_general | solution.py:86
  841.6 4.1 multiply_subtract_fusion
  845.7 3.5 fusion.18
  849.2 4.1 fusion.3
  853.3 3.9 fusion.19
  857.3 4.1 fusion.2
  861.4 3.5 fusion.20
  864.9 4.3 fusion.1
  869.2 3.5 fusion.21
  872.8 5.1 fusion.6
  (6 shorter events, 0.0 us)
Async XLA Ops:
  254.2 302.8 %all-to-all-start.1 = ((bf16[16,1,128,4096]{3,2,1,0:T(8,128)(2,1)}), bf16[16,1,128,4096]{3,2,1,0:T(8,128)(2,1)}, u32[]{:S(2)}, u32[]{:S(2)}) async-start(bf16[16,1,128,4096]{3,2,1,0:T(8,128)(2,1)} %get-tuple-element.8), calls=%async_computation.1 | async-start | bytes 33554432 | tf_op jit(solution)/shard_map/all_to_all | solution.py:38
  259.4 320.5 %all-gather.2.cloned.1.call-start = ((), (), s32[]{:S(2)}) async-start(), calls=%async_computation.2 | async-start | bytes 2359296 | tf_op jit(solution)/shard_map/all_gather | solution.py:63
  627.4 7.4 collective-permute-start
  637.5 96.5 %copy-start.1 = (bf16[1,256,4096]{2,1,0:T(8,128)(2,1)S(1)}, bf16[1,256,4096]{2,1,0:T(8,128)(2,1)}, u32[]{:S(2)}) copy-start(bf16[1,256,4096]{2,1,0:T(8,128)(2,1)} %all-gather.2.cloned.1.call-done) | copy-start | bytes 6291460
  637.5 92.7 %collective-permute-start.1 = (f32[256,4096]{1,0:T(8,128)S(1)}, f32[256,4096]{1,0:T(8,128)S(1)}, u32[]{:S(2)}, u32[]{:S(2)}) collective-permute-start(f32[256,4096]{1,0:T(8,128)S(1)} %add.25), channel_id=1, source_target_pairs={{0,32},{16,48},{32,0},{48,16},{64,96},{80,112},{96,64},{112,80},{1... | collective-permute-start | bytes 12582920 | tf_op jit(solution)/shard_map/ppermute | solution.py:75
  730.7 93.6 %collective-permute-start.2 = (f32[256,4096]{1,0:T(8,128)S(1)}, f32[256,4096]{1,0:T(8,128)S(1)}, u32[]{:S(2)}, u32[]{:S(2)}) collective-permute-start(f32[256,4096]{1,0:T(8,128)S(1)} %add.26), channel_id=1, source_target_pairs={{0,64},{16,80},{32,96},{48,112},{64,0},{80,16},{96,32},{112,48},{1... | collective-permute-start | bytes 12582920 | tf_op jit(solution)/shard_map/ppermute | solution.py:75
  829.3 12.2 %copy-start = (f32[256,4096]{1,0:T(8,128)S(1)}, f32[256,4096]{1,0:T(8,128)}, u32[]{:S(2)}) copy-start(f32[256,4096]{1,0:T(8,128)} %get-tuple-element.6) | copy-start | bytes 12582916
Sparse Core Ops, SparseCore 0:
  261.9 26.6 all-gather.1
